TPU v7x, 32 devices: a whole 2x2x4 slice. The times are simulated.
32 devices in a mesh: samp: 4 (over x, core), snp: 8 (over z, y).
Axes of the slice: x: 2, y: 2, z: 4, core: 2. Of those that a mesh axis runs over, the one named last changes fastest.
Arguments:
- genotype: bfloat16 [40960, 40960], P('samp', 'snp'), may hold values from 0 to 2, as said below
- centre: float32 [40960], P('snp'), may hold values from 0.1 to 1
- spread: float32 [40960], P('snp'), may hold values from 0.308 to 0.7072
- pheno_probes: float32 [32, 40960], P(None, ('samp', 'snp')), may hold values from -15.75 to 15.75
Outputs:
- solution: float32 [32, 40960], P(None, ('samp', 'snp'))
- marker_stats: float32 [32, 40960], P(None, 'snp')
Inputs may be any that keep to these rules, and one draw needn't show every extreme that they name: `genotype`: whole numbers.
All inputs are finite; a program needn't handle non-finite values.
Results may differ from a plain program's by a relative error of at most 0.0003.
Values sent between devices are 32-bit elements; how exact they have to be, the bound alone decides.
A program may use at most 448 MiB of HBM per device.

v0:
```python
import math
import jax
import jax.numpy as jnp
from jax import lax
from jax.sharding import PartitionSpec as P

ROUNDS = 3
RIDGE = 0.1
LANES = 128


def split(values):
    high = lax.reduce_precision(values, 8, 7)
    low = lax.reduce_precision(values - high, 8, 7)
    return (jnp.concatenate([high, low], axis=0).astype(jnp.bfloat16), high + low)


def product(pieces, genotype, dimension):
    rows = pieces.shape[0] // 2
    pieces = lax.dot_general(
        pieces, genotype, (((1,), (dimension,)), ((), ())), preferred_element_type=jnp.float32
    )
    return pieces[:rows] + pieces[rows:]


def row_sum(values):
    return jnp.sum(values, axis=1, keepdims=True)


def with_scalars(values, scalars):
    rows = values.shape[0]
    filler = jnp.zeros((rows, LANES - len(scalars)), jnp.float32)
    return jnp.concatenate([values, *scalars, filler], axis=1)


def local(samples, markers, genotype, centre, spread, pheno_probes):
    shard = pheno_probes.shape[1]
    columns = genotype.shape[1]
    block = genotype.shape[0]
    first = lax.axis_index("snp") * shard
    inverse = 1.0 / spread[None, :]
    middle = centre[None, :]
    residual = lax.all_gather(pheno_probes, "snp", axis=1, tiled=True)
    direction = load = norm = square = None
    solution = stats = None
    for counter in range(ROUNDS):
        pieces, rounded = split(residual)
        scalars = [row_sum(rounded), row_sum(residual * residual)]
        if counter:
            scalars.append(row_sum(residual * direction))
        raw = product(pieces, genotype, 0)
        total = lax.psum(with_scalars(raw, scalars), "samp")
        residual_load = (total[:, :columns] - total[:, columns : columns + 1] * middle) * inverse
        norm_next = total[:, columns + 1 : columns + 2]
        if counter:
            ratio = norm_next / norm
            cross = total[:, columns + 2 : columns + 3]
            load = residual_load + ratio * load
            direction = residual + ratio * direction
            square = norm_next + 2.0 * ratio * cross + ratio * ratio * square
        else:
            load, direction, square = (residual_load, residual, norm_next)
        norm = norm_next
        power = row_sum(load * load)
        if counter < ROUNDS - 1:
            pieces, rounded = split(load * inverse)
            image = product(pieces, genotype, 1) - row_sum(rounded * middle)
            summed = lax.psum(with_scalars(image, [power]), "snp")
            power = summed[:, block : block + 1]
        else:
            power = lax.psum(power, "snp")
        step = norm / (power / markers + RIDGE * square)
        own = lax.dynamic_slice_in_dim(direction, first, shard, 1)
        solution = step * own if solution is None else solution + step * own
        stats = step * load if stats is None else stats + step * load
        if counter < ROUNDS - 1:
            applied = summed[:, :block] / markers + RIDGE * direction
            residual = residual - step * applied
    return (solution, stats / math.sqrt(samples))


def solution(mesh):
    in_specs = (P("samp", "snp"), P("snp"), P("snp"), P(None, ("samp", "snp")))
    out_specs = (P(None, ("samp", "snp")), P(None, "snp"))

    def whole(genotype, centre, spread, pheno_probes):
        samples, markers = genotype.shape

        def body(*blocks):
            return local(samples, markers, *blocks)

        return jax.shard_map(
            body, mesh=mesh, in_specs=in_specs, out_specs=out_specs, check_vma=False
        )(genotype, centre, spread, pheno_probes)

    return whole
```

profile of v0, /device:TPU:0, one launch (start us, length us, event | category | flops | bytes accessed | tf_op | source)
XLA Modules:
  0.0 597.3 jit_solution(6193682254995479344)
XLA Ops:
  7.2 0.0 all-gather.2.cloned.1.call-start
  7.2 0.7 all-gather.2.cloned.1.call-update
  7.9 0.0 all-reduce.6.cloned.1.call-start
  7.9 46.8 %all-gather.2.cloned.1.call-done = f32[32,10240]{1,0:T(8,128)} async-done(((f32[32,1280]{1,0:T(8,128)}), f32[32,10240]{1,0:T(8,128)}) %all-gather.2.cloned.1.call-update) | async-done | bytes 1310736 | tf_op jit(solution)/shard_map/all_gather | solution.py:43
  54.7 1.8 multiply_reduce_fusion.4
  56.5 35.8 %fusion.17 = f32[64,5120]{1,0:T(8,128)S(1)} fusion(bf16[10240,5120]{1,0:T(8,128)(2,1)} %param.4, bf16[32,10240]{1,0:T(8,128)(2,1)S(1)} %get-tuple-element.26, bf16[32,10240]{1,0:T(8,128)(2,1)S(1)} %get-tuple-element.27), kind=kOutput, calls=%fused_computation.30 | convolution fusion | flops 6713507840 | bytes 107479040 | tf_op jit(solution)/shard_map/dot_general | solution.py:20
  92.3 0.1 slice_add_fusion.4
  92.4 0.0 copy-start.4
  92.4 0.1 copy.17
  92.5 0.1 copy.18
  92.6 0.9 concatenate.36
  93.5 0.0 all-reduce.6.cloned.1.call-update
  93.5 0.0 all-reduce.8.cloned.1.call-start
  93.6 32.9 %all-reduce.6.cloned.1.call-done = f32[32,5248]{1,0:T(8,128)} async-done(((f32[32,5248]{1,0:T(8,128)}), f32[32,5248]{1,0:T(8,128)}) %all-reduce.6.cloned.1.call-update) | async-done | bytes 671760 | tf_op jit(solution)/shard_map/psum | solution.py:52
  126.4 0.8 slice_reduce_fusion.2
  127.3 1.5 multiply_reduce_fusion.7
  128.8 0.1 copy.19
  128.9 39.7 %fusion.42 = f32[64,10240]{1,0:T(8,128)S(1)} fusion(bf16[10240,5120]{1,0:T(8,128)(2,1)} %param.4, bf16[32,5120]{1,0:T(8,128)(2,1)S(1)} %get-tuple-element.29, bf16[32,5120]{1,0:T(8,128)(2,1)S(1)} %get-tuple-element.28), kind=kOutput, calls=%fused_computation.73 | convolution fusion | flops 6712197120 | bytes 108134400 | tf_op jit(solution)/shard_map/dot_general | solution.py:20
  168.6 1.2 fusion.16
  169.8 2.3 concatenate.38
  172.1 0.0 all-reduce.8.cloned.1.call-update
  172.1 0.0 all-reduce.10.cloned.1.call-start
  172.2 84.1 %all-reduce.8.cloned.1.call-done = f32[32,10368]{1,0:T(8,128)} async-done(((f32[32,10368]{1,0:T(8,128)}), f32[32,10368]{1,0:T(8,128)}) %all-reduce.8.cloned.1.call-update) | async-done | bytes 1327120 | tf_op jit(solution)/shard_map/psum | solution.py:68
  256.3 0.9 fusion.63
  257.2 2.1 multiply_reduce_fusion.2
  259.3 1.0 reduce-precision_convert_fusion.1
  260.3 37.0 %fusion.21 = f32[64,5120]{1,0:T(8,128)} fusion(bf16[10240,5120]{1,0:T(8,128)(2,1)} %param.4, bf16[32,10240]{1,0:T(8,128)(2,1)} %get-tuple-element.25, bf16[32,10240]{1,0:T(8,128)(2,1)S(1)} %get-tuple-element.24), kind=kOutput, calls=%fused_computation.34 | convolution fusion | flops 6713507840 | bytes 107479040 | tf_op jit(solution)/shard_map/dot_general | solution.py:20
  297.3 1.4 slice_add_fusion.3
  298.7 0.1 copy.20
  298.8 0.1 copy.21
  298.9 0.1 copy.22
  299.0 0.9 concatenate.40
  299.9 0.0 all-reduce.10.cloned.1.call-update
  299.9 0.2 all-reduce.12.cloned.1.call-start
  300.1 33.0 %all-reduce.10.cloned.1.call-done = f32[32,5248]{1,0:T(8,128)} async-done(((f32[32,5248]{1,0:T(8,128)}), f32[32,5248]{1,0:T(8,128)}) %all-reduce.10.cloned.1.call-update) | async-done | bytes 671760 | tf_op jit(solution)/shard_map/psum | solution.py:52
  333.1 1.0 slice_reduce_fusion.1
  334.1 1.8 multiply_reduce_fusion.6
  336.0 0.9 reduce-precision_convert_fusion.3
  336.9 0.1 copy.23
  337.0 40.9 %fusion.46 = f32[64,10240]{1,0:T(8,128)} fusion(bf16[10240,5120]{1,0:T(8,128)(2,1)} %param.4, bf16[32,5120]{1,0:T(8,128)(2,1)} %get-tuple-element.31, bf16[32,5120]{1,0:T(8,128)(2,1)} %get-tuple-element.30), kind=kOutput, calls=%fused_computation.77 | convolution fusion | flops 6712197120 | bytes 108134400 | tf_op jit(solution)/shard_map/dot_general | solution.py:20
  377.9 3.0 fusion.12
  380.9 2.3 concatenate.42
  383.1 0.0 all-reduce.12.cloned.1.call-update
  383.2 0.0 all-reduce.14.cloned.1.call-start
  383.2 84.1 %all-reduce.12.cloned.1.call-done = f32[32,10368]{1,0:T(8,128)} async-done(((f32[32,10368]{1,0:T(8,128)}), f32[32,10368]{1,0:T(8,128)}) %all-reduce.12.cloned.1.call-update) | async-done | bytes 1327120 | tf_op jit(solution)/shard_map/psum | solution.py:68
  467.3 1.0 fusion.64
  468.3 3.3 multiply_reduce_fusion
  471.6 1.4 reduce-precision_convert_fusion
  473.0 0.1 copy-done.2
  473.1 36.2 %fusion.25 = f32[64,5120]{1,0:T(8,128)S(1)} fusion(bf16[10240,5120]{1,0:T(8,128)(2,1)} %param.4, bf16[32,10240]{1,0:T(8,128)(2,1)} %get-tuple-element.23, bf16[32,10240]{1,0:T(8,128)(2,1)} %get-tuple-element.22), kind=kOutput, calls=%fused_computation.38 | convolution fusion | flops 6713507840 | bytes 107479040 | tf_op jit(solution)/shard_map/dot_general | solution.py:20
  509.3 0.9 slice_add_fusion.2
  510.2 0.1 copy.24
  510.3 0.1 copy.25
  510.4 0.1 copy.26
  510.5 2.1 concatenate.44
  512.5 0.0 all-reduce.14.cloned.1.call-update
  512.5 33.2 %all-reduce.14.cloned.1.call-done = f32[32,5248]{1,0:T(8,128)} async-done(((f32[32,5248]{1,0:T(8,128)}), f32[32,5248]{1,0:T(8,128)}) %all-reduce.14.cloned.1.call-update) | async-done | bytes 671760 | tf_op jit(solution)/shard_map/psum | solution.py:52
  545.8 1.0 slice_reduce_fusion
  546.7 1.4 multiply_reduce_fusion.5
  548.2 0.1 copy.27
  548.3 37.1 %psum.47 = f32[32,1]{1,0:T(8,128)S(1)} all-reduce(f32[32,1]{1,0:T(8,128)S(1)} %copy.27), channel_id=1, replica_groups=mesh['samp'=4,'snp'=8] {'snp'}, use_global_device_ids=true, to_apply=%region_18.0 | all-reduce | flops 32 | bytes 256 | tf_op jit(solution)/shard_map/psum | solution.py:71
  585.3 1.0 fusion.65
  586.3 2.3 add_multiply_fusion
  588.6 1.8 fusion.51
  (12 shorter events, 0.0 us)
Async XLA Ops:
  7.2 47.5 %all-gather.2.cloned.1.call-start = ((), (), s32[]{:S(2)}) async-start(), calls=%async_computation | async-start | bytes 1474560 | tf_op jit(solution)/shard_map/all_gather | solution.py:43
  7.9 118.5 %all-reduce.6.cloned.1.call-start = ((), (), s32[]{:S(2)}) async-start(), calls=%async_computation.1 | async-start | bytes 1343488 | tf_op jit(solution)/shard_map/psum | solution.py:52
  92.4 1.2 copy-start.4
  92.4 34.9 %copy-start.3 = (f32[5120]{0:T(1024)S(1)}, f32[5120]{0:T(1024)}, u32[]{:S(2)}) copy-start(f32[5120]{0:T(1024)} %param.5) | copy-start | bytes 61444
  93.5 162.8 %all-reduce.8.cloned.1.call-start = ((), (), s32[]{:S(2)}) async-start(), calls=%async_computation.2 | async-start | bytes 2654208 | tf_op jit(solution)/shard_map/psum | solution.py:68
  172.1 85.1 %copy-start = (f32[32,10240]{1,0:T(8,128)S(1)}, f32[32,10240]{1,0:T(8,128)}, u32[]{:S(2)}) copy-start(f32[32,10240]{1,0:T(8,128)} %all-gather.2.cloned.1.call-done) | copy-start | bytes 3932164
  172.1 161.0 %all-reduce.10.cloned.1.call-start = ((), (), s32[]{:S(2)}) async-start(), calls=%async_computation.3 | async-start | bytes 1343488 | tf_op jit(solution)/shard_map/psum | solution.py:52
  299.9 167.4 %all-reduce.12.cloned.1.call-start = ((), (), s32[]{:S(2)}) async-start(), calls=%async_computation.4 | async-start | bytes 2654208 | tf_op jit(solution)/shard_map/psum | solution.py:68
  383.2 162.6 %all-reduce.14.cloned.1.call-start = ((), (), s32[]{:S(2)}) async-start(), calls=%async_computation.5 | async-start | bytes 1343488 | tf_op jit(solution)/shard_map/psum | solution.py:52
  471.6 1.5 copy-start.2
  512.5 72.8 %copy-start.1 = (f32[32,5248]{1,0:T(8,128)S(1)}, f32[32,5248]{1,0:T(8,128)}, u32[]{:S(2)}) copy-start(f32[32,5248]{1,0:T(8,128)} %all-reduce.6.cloned.1.call-done) | copy-start | bytes 2015236
Sparse Core Ops, SparseCore 0:
  10.2 44.5 all-gather.1
  93.6 32.7 all-reduce.5
  172.2 84.0 all-reduce.7
  300.0 33.0 all-reduce.9
  383.3 83.9 all-reduce.11
  512.7 33.0 all-reduce.13
where the time goes:
time: 599 us; the launch traced here: 597 us
  waiting for transfers between devices  315 us (53%)
  matrix products  190 us (32%)
  blocking collectives  37.1 us (6%)
  other arithmetic  30.7 us (5%)
  between operations  14.2 us (2%)
  local copies, waits for them, and re-layouts  10.3 us (2%)
    dot_general x5, matrix products, product(): lax.dot_general(pieces, genotype, (((1,), (dimension,)), ((), ())), prefe...  190 us
    psum x2, waiting for transfers between devices, local(): summed = lax.psum(with_scalars(image, [power]), 'snp')  168 us
    psum x3, waiting for transfers between devices, local(): total = lax.psum(with_scalars(raw, scalars), 'samp')  99.1 us
    all_gather x1, waiting for transfers between devices, local(): residual = lax.all_gather(pheno_probes, 'snp', axis=1, tiled=True)  46.8 us
    psum x1, blocking collectives, local(): power = lax.psum(power, 'snp')  37.1 us
  transfers between devices with their start and end apart: 6, of which 6 were waited for; matrix products, arithmetic and copies ran while one was open for 0% of the time, Pallas kernels for 0%

commit v1 on v0

--- a/solution.py
+++ b/solution.py
@@ -40,7 +40,12 @@
     first = lax.axis_index("snp") * shard
     inverse = 1.0 / spread[None, :]
     middle = centre[None, :]
-    residual = lax.all_gather(pheno_probes, "snp", axis=1, tiled=True)
+    ring = [pheno_probes]
+    for hop in range(7):
+        ring.append(lax.ppermute(ring[-1], "snp", [(dev, (dev + 1) % 8) for dev in range(8)]))
+    residual = jnp.roll(
+        jnp.concatenate(ring[::-1], axis=1), (lax.axis_index("snp") + 1) * ring[0].shape[1], axis=1
+    )
     direction = load = norm = square = None
     solution = stats = None
     for counter in range(ROUNDS):

time: 599 us -> 606 us (1.012)
  waiting for transfers between devices: 315 us -> 323 us
    ppermute x0 -> x7, waiting for transfers between devices: none -> 56.5 us  [local(): lax.ppermute(ring[-1], 'snp', [(dev, (dev + 1) % 8) for dev in range(8)])]
    all_gather x1 -> x0, waiting for transfers between devices: 46.8 us -> none  [local(): residual = lax.all_gather(pheno_probes, 'snp', axis=1, tiled=True)]
  transfers between devices with their start and end apart: 6 -> 12, of which waited for: 6 -> 12; matrix products, arithmetic and copies ran while one was open for 0% -> 0% of each run, Pallas kernels for 0% -> 0%
where the time goes in v1:
time: 606 us; the launch traced here: 605 us
  waiting for transfers between devices  323 us (53%)
  matrix products  191 us (32%)
  blocking collectives  37.1 us (6%)
  other arithmetic  26.6 us (4%)
  between operations  14.1 us (2%)
  local copies, waits for them, and re-layouts  10.5 us (2%)
    dot_general x5, matrix products, product(): lax.dot_general(pieces, genotype, (((1,), (dimension,)), ((), ())), prefe...  191 us
    psum x2, waiting for transfers between devices, local(): summed = lax.psum(with_scalars(image, [power]), 'snp')  168 us
    psum x3, waiting for transfers between devices, local(): total = lax.psum(with_scalars(raw, scalars), 'samp')  98.4 us
    ppermute x7, waiting for transfers between devices, local(): lax.ppermute(ring[-1], 'snp', [(dev, (dev + 1) % 8) for dev in range(8)])  56.5 us
    psum x1, blocking collectives, local(): power = lax.psum(power, 'snp')  37.1 us
  transfers between devices with their start and end apart: 12, of which 12 were waited for; matrix products, arithmetic and copies ran while one was open for 0% of the time, Pallas kernels for 0%

profile of v1, /device:TPU:0, one launch (start us, length us, event | category | flops | bytes accessed | tf_op | source)
XLA Modules:
  0.0 605.4 jit_solution(8926649795794939985)
XLA Ops:
  7.2 0.0 all-reduce.6.cloned.1.call-start
  7.2 3.0 collective-permute-start
  10.3 7.4 %collective-permute-done = f32[32,1280]{1,0:T(8,128)S(1)} collective-permute-done((f32[32,1280]{1,0:T(8,128)}, f32[32,1280]{1,0:T(8,128)S(1)}, u32[]{:S(2)}, u32[]{:S(2)}) %collective-permute-start) | collective-permute-done | bytes 163872 | tf_op jit(solution)/shard_map/ppermute | solution.py:45
  17.7 8.1 %collective-permute-done.1 = f32[32,1280]{1,0:T(8,128)S(1)} collective-permute-done((f32[32,1280]{1,0:T(8,128)S(1)}, f32[32,1280]{1,0:T(8,128)S(1)}, u32[]{:S(2)}, u32[]{:S(2)}) %collective-permute-start.1) | collective-permute-done | bytes 163872 | tf_op jit(solution)/shard_map/ppermute | solution.py:45
  25.8 8.0 %collective-permute-done.2 = f32[32,1280]{1,0:T(8,128)S(1)} collective-permute-done((f32[32,1280]{1,0:T(8,128)S(1)}, f32[32,1280]{1,0:T(8,128)S(1)}, u32[]{:S(2)}, u32[]{:S(2)}) %collective-permute-start.2) | collective-permute-done | bytes 163872 | tf_op jit(solution)/shard_map/ppermute | solution.py:45
  33.8 8.0 %collective-permute-done.3 = f32[32,1280]{1,0:T(8,128)S(1)} collective-permute-done((f32[32,1280]{1,0:T(8,128)S(1)}, f32[32,1280]{1,0:T(8,128)S(1)}, u32[]{:S(2)}, u32[]{:S(2)}) %collective-permute-start.3) | collective-permute-done | bytes 163872 | tf_op jit(solution)/shard_map/ppermute | solution.py:45
  41.8 8.0 %collective-permute-done.4 = f32[32,1280]{1,0:T(8,128)S(1)} collective-permute-done((f32[32,1280]{1,0:T(8,128)S(1)}, f32[32,1280]{1,0:T(8,128)S(1)}, u32[]{:S(2)}, u32[]{:S(2)}) %collective-permute-start.4) | collective-permute-done | bytes 163872 | tf_op jit(solution)/shard_map/ppermute | solution.py:45
  49.8 8.9 %collective-permute-done.5 = f32[32,1280]{1,0:T(8,128)S(1)} collective-permute-done((f32[32,1280]{1,0:T(8,128)S(1)}, f32[32,1280]{1,0:T(8,128)S(1)}, u32[]{:S(2)}, u32[]{:S(2)}) %collective-permute-start.5) | collective-permute-done | bytes 163872 | tf_op jit(solution)/shard_map/ppermute | solution.py:45
  58.7 8.0 %collective-permute-done.6 = f32[32,1280]{1,0:T(8,128)S(1)} collective-permute-done((f32[32,1280]{1,0:T(8,128)S(1)}, f32[32,1280]{1,0:T(8,128)S(1)}, u32[]{:S(2)}, u32[]{:S(2)}) %collective-permute-start.6) | collective-permute-done | bytes 163872 | tf_op jit(solution)/shard_map/ppermute | solution.py:45
  67.1 0.6 multiply_reduce_fusion.4
  67.7 0.9 copy-done
  68.6 35.8 %fusion.17 = f32[64,5120]{1,0:T(8,128)S(1)} fusion(bf16[10240,5120]{1,0:T(8,128)(2,1)} %param.4, bf16[32,10240]{1,0:T(8,128)(2,1)S(1)} %get-tuple-element.22, bf16[32,10240]{1,0:T(8,128)(2,1)S(1)} %get-tuple-element.23), kind=kOutput, calls=%fused_computation.30 | convolution fusion | flops 6713507840 | bytes 107479040 | tf_op jit(solution)/shard_map/dot_general | solution.py:20
  104.4 0.1 slice_add_fusion.4
  104.5 0.1 copy.17
  104.6 0.1 copy.18
  104.7 0.9 concatenate.43
  105.6 0.0 all-reduce.8.cloned.1.call-start
  105.7 32.0 %all-reduce.6.cloned.1.call-done = f32[32,5248]{1,0:T(8,128)} async-done(((f32[32,5248]{1,0:T(8,128)}), f32[32,5248]{1,0:T(8,128)}) %all-reduce.6.cloned.1.call-update) | async-done | bytes 671760 | tf_op jit(solution)/shard_map/psum | solution.py:57
  137.7 0.8 slice_reduce_fusion.2
  138.5 1.5 multiply_reduce_fusion.7
  140.1 0.1 copy.19
  140.1 39.7 %fusion.42 = f32[64,10240]{1,0:T(8,128)S(1)} fusion(bf16[10240,5120]{1,0:T(8,128)(2,1)} %param.4, bf16[32,5120]{1,0:T(8,128)(2,1)S(1)} %get-tuple-element.29, bf16[32,5120]{1,0:T(8,128)(2,1)S(1)} %get-tuple-element.28), kind=kOutput, calls=%fused_computation.73 | convolution fusion | flops 6712197120 | bytes 108134400 | tf_op jit(solution)/shard_map/dot_general | solution.py:20
  179.8 1.2 fusion.16
  181.1 2.3 concatenate.45
  183.4 0.2 all-reduce.10.cloned.1.call-start
  183.6 83.9 %all-reduce.8.cloned.1.call-done = f32[32,10368]{1,0:T(8,128)} async-done(((f32[32,10368]{1,0:T(8,128)}), f32[32,10368]{1,0:T(8,128)}) %all-reduce.8.cloned.1.call-update) | async-done | bytes 1327120 | tf_op jit(solution)/shard_map/psum | solution.py:73
  267.5 0.9 fusion.63
  268.4 2.6 multiply_reduce_fusion.2
  271.0 0.2 reduce-precision_convert_fusion.1
  271.2 36.9 %fusion.21 = f32[64,5120]{1,0:T(8,128)} fusion(bf16[10240,5120]{1,0:T(8,128)(2,1)} %param.4, bf16[32,10240]{1,0:T(8,128)(2,1)S(1)} %get-tuple-element.27, bf16[32,10240]{1,0:T(8,128)(2,1)S(1)} %get-tuple-element.26), kind=kOutput, calls=%fused_computation.34 | convolution fusion | flops 6713507840 | bytes 107479040 | tf_op jit(solution)/shard_map/dot_general | solution.py:20
  308.1 1.4 slice_add_fusion.3
  309.5 0.1 copy.20
  309.5 0.1 copy.21
  309.6 0.1 copy.22
  309.7 0.9 concatenate.47
  310.7 0.0 all-reduce.12.cloned.1.call-start
  310.7 33.2 %all-reduce.10.cloned.1.call-done = f32[32,5248]{1,0:T(8,128)} async-done(((f32[32,5248]{1,0:T(8,128)}), f32[32,5248]{1,0:T(8,128)}) %all-reduce.10.cloned.1.call-update) | async-done | bytes 671760 | tf_op jit(solution)/shard_map/psum | solution.py:57
  343.9 1.0 slice_reduce_fusion.1
  344.9 1.6 multiply_reduce_fusion.6
  346.5 0.1 reduce-precision_convert_fusion.3
  346.6 0.1 copy.23
  346.7 42.4 %fusion.46 = f32[64,10240]{1,0:T(8,128)} fusion(bf16[10240,5120]{1,0:T(8,128)(2,1)} %param.4, bf16[32,5120]{1,0:T(8,128)(2,1)S(1)} %get-tuple-element.31, bf16[32,5120]{1,0:T(8,128)(2,1)S(1)} %get-tuple-element.30), kind=kOutput, calls=%fused_computation.77 | convolution fusion | flops 6712197120 | bytes 108134400 | tf_op jit(solution)/shard_map/dot_general | solution.py:20
  389.1 3.0 fusion.12
  392.0 2.2 concatenate.49
  394.3 0.3 all-reduce.14.cloned.1.call-start
  394.6 83.9 %all-reduce.12.cloned.1.call-done = f32[32,10368]{1,0:T(8,128)} async-done(((f32[32,10368]{1,0:T(8,128)}), f32[32,10368]{1,0:T(8,128)}) %all-reduce.12.cloned.1.call-update) | async-done | bytes 1327120 | tf_op jit(solution)/shard_map/psum | solution.py:73
  478.5 1.0 fusion.64
  479.5 3.7 multiply_reduce_fusion
  483.2 1.1 reduce-precision_convert_fusion
  484.4 0.2 copy-done.2
  484.6 36.0 %fusion.25 = f32[64,5120]{1,0:T(8,128)S(1)} fusion(bf16[10240,5120]{1,0:T(8,128)(2,1)} %param.4, bf16[32,10240]{1,0:T(8,128)(2,1)} %get-tuple-element.25, bf16[32,10240]{1,0:T(8,128)(2,1)S(1)} %get-tuple-element.24), kind=kOutput, calls=%fused_computation.38 | convolution fusion | flops 6713507840 | bytes 107479040 | tf_op jit(solution)/shard_map/dot_general | solution.py:20
  520.6 0.1 slice_add_fusion.2
  520.7 0.1 copy.24
  520.7 0.1 copy.25
  520.8 0.1 copy.26
  520.9 0.9 concatenate.51
  521.9 33.2 %all-reduce.14.cloned.1.call-done = f32[32,5248]{1,0:T(8,128)} async-done(((f32[32,5248]{1,0:T(8,128)}), f32[32,5248]{1,0:T(8,128)}) %all-reduce.14.cloned.1.call-update) | async-done | bytes 671760 | tf_op jit(solution)/shard_map/psum | solution.py:57
  555.1 1.0 slice_reduce_fusion
  556.2 1.4 multiply_reduce_fusion.5
  557.6 0.1 copy.27
  557.7 37.1 %psum.47 = f32[32,1]{1,0:T(8,128)S(1)} all-reduce(f32[32,1]{1,0:T(8,128)S(1)} %copy.27), channel_id=1, replica_groups=mesh['samp'=4,'snp'=8] {'snp'}, use_global_device_ids=true, to_apply=%region_18.19 | all-reduce | flops 32 | bytes 256 | tf_op jit(solution)/shard_map/psum | solution.py:76
  594.8 1.0 fusion.65
  595.8 1.9 fusion.51
  597.7 1.2 add_multiply_fusion
  (43 shorter events, 0.4 us)
Async XLA Ops:
  7.2 59.7 %copy-start.4 = (f32[32,1280]{1,0:T(8,128)S(1)}, f32[32,1280]{1,0:T(8,128)}, u32[]{:S(2)}) copy-start(f32[32,1280]{1,0:T(8,128)} %param.7) | copy-start | bytes 491524
  7.2 130.5 %all-reduce.6.cloned.1.call-start = ((), (), s32[]{:S(2)}) async-start(), calls=%async_computation | async-start | bytes 1343488 | tf_op jit(solution)/shard_map/psum | solution.py:57
  7.2 10.5 %collective-permute-start = (f32[32,1280]{1,0:T(8,128)}, f32[32,1280]{1,0:T(8,128)S(1)}, u32[]{:S(2)}, u32[]{:S(2)}) collective-permute-start(f32[32,1280]{1,0:T(8,128)} %param.7), channel_id=1, source_target_pairs={{0,1},{1,2},{2,3},{3,4},{4,5},{5,6},{6,7},{7,0},{8,9},{9,10},{10,1... | collective-permute-start | bytes 491528 | tf_op jit(solution)/shard_map/ppermute | solution.py:45
  17.7 8.1 %collective-permute-start.1 = (f32[32,1280]{1,0:T(8,128)S(1)}, f32[32,1280]{1,0:T(8,128)S(1)}, u32[]{:S(2)}, u32[]{:S(2)}) collective-permute-start(f32[32,1280]{1,0:T(8,128)S(1)} %collective-permute-done), channel_id=1, source_target_pairs={{0,1},{1,2},{2,3},{3,4},{4,5},{5,6},{6,7},{7,0},{8,9},{9,10},{10,1... | collective-permute-start | bytes 491528 | tf_op jit(solution)/shard_map/ppermute | solution.py:45
  25.8 8.0 %collective-permute-start.2 = (f32[32,1280]{1,0:T(8,128)S(1)}, f32[32,1280]{1,0:T(8,128)S(1)}, u32[]{:S(2)}, u32[]{:S(2)}) collective-permute-start(f32[32,1280]{1,0:T(8,128)S(1)} %collective-permute-done.1), channel_id=1, source_target_pairs={{0,1},{1,2},{2,3},{3,4},{4,5},{5,6},{6,7},{7,0},{8,9},{9,10},{10,1... | collective-permute-start | bytes 491528 | tf_op jit(solution)/shard_map/ppermute | solution.py:45
  33.8 8.0 %collective-permute-start.3 = (f32[32,1280]{1,0:T(8,128)S(1)}, f32[32,1280]{1,0:T(8,128)S(1)}, u32[]{:S(2)}, u32[]{:S(2)}) collective-permute-start(f32[32,1280]{1,0:T(8,128)S(1)} %collective-permute-done.2), channel_id=1, source_target_pairs={{0,1},{1,2},{2,3},{3,4},{4,5},{5,6},{6,7},{7,0},{8,9},{9,10},{10,1... | collective-permute-start | bytes 491528 | tf_op jit(solution)/shard_map/ppermute | solution.py:45
  41.8 8.0 %collective-permute-start.4 = (f32[32,1280]{1,0:T(8,128)S(1)}, f32[32,1280]{1,0:T(8,128)S(1)}, u32[]{:S(2)}, u32[]{:S(2)}) collective-permute-start(f32[32,1280]{1,0:T(8,128)S(1)} %collective-permute-done.3), channel_id=1, source_target_pairs={{0,1},{1,2},{2,3},{3,4},{4,5},{5,6},{6,7},{7,0},{8,9},{9,10},{10,1... | collective-permute-start | bytes 491528 | tf_op jit(solution)/shard_map/ppermute | solution.py:45
  49.8 8.9 %collective-permute-start.5 = (f32[32,1280]{1,0:T(8,128)S(1)}, f32[32,1280]{1,0:T(8,128)S(1)}, u32[]{:S(2)}, u32[]{:S(2)}) collective-permute-start(f32[32,1280]{1,0:T(8,128)S(1)} %collective-permute-done.4), channel_id=1, source_target_pairs={{0,1},{1,2},{2,3},{3,4},{4,5},{5,6},{6,7},{7,0},{8,9},{9,10},{10,1... | collective-permute-start | bytes 491528 | tf_op jit(solution)/shard_map/ppermute | solution.py:45
  58.7 8.0 %collective-permute-start.6 = (f32[32,1280]{1,0:T(8,128)S(1)}, f32[32,1280]{1,0:T(8,128)S(1)}, u32[]{:S(2)}, u32[]{:S(2)}) collective-permute-start(f32[32,1280]{1,0:T(8,128)S(1)} %collective-permute-done.5), channel_id=1, source_target_pairs={{0,1},{1,2},{2,3},{3,4},{4,5},{5,6},{6,7},{7,0},{8,9},{9,10},{10,1... | collective-permute-start | bytes 491528 | tf_op jit(solution)/shard_map/ppermute | solution.py:45
  67.1 1.5 copy-start
  104.5 1.2 copy-start.6
  104.5 34.0 %copy-start.5 = (f32[5120]{0:T(1024)S(1)}, f32[5120]{0:T(1024)}, u32[]{:S(2)}) copy-start(f32[5120]{0:T(1024)} %param.5) | copy-start | bytes 61444
  105.6 161.9 %all-reduce.8.cloned.1.call-start = ((), (), s32[]{:S(2)}) async-start(), calls=%async_computation.1 | async-start | bytes 2654208 | tf_op jit(solution)/shard_map/psum | solution.py:73
  183.4 84.2 %copy-start.1 = (f32[32,5248]{1,0:T(8,128)S(1)}, f32[32,5248]{1,0:T(8,128)}, u32[]{:S(2)}) copy-start(f32[32,5248]{1,0:T(8,128)} %all-reduce.6.cloned.1.call-done) | copy-start | bytes 2015236
  183.4 160.5 %all-reduce.10.cloned.1.call-start = ((), (), s32[]{:S(2)}) async-start(), calls=%async_computation.2 | async-start | bytes 1343488 | tf_op jit(solution)/shard_map/psum | solution.py:57
  310.7 167.8 %all-reduce.12.cloned.1.call-start = ((), (), s32[]{:S(2)}) async-start(), calls=%async_computation.3 | async-start | bytes 2654208 | tf_op jit(solution)/shard_map/psum | solution.py:73
  394.3 160.8 %all-reduce.14.cloned.1.call-start = ((), (), s32[]{:S(2)}) async-start(), calls=%async_computation.4 | async-start | bytes 1343488 | tf_op jit(solution)/shard_map/psum | solution.py:57
  483.2 1.4 copy-start.2
  555.1 39.6 %copy-start.3 = (f32[32,5248]{1,0:T(8,128)S(1)}, f32[32,5248]{1,0:T(8,128)}, u32[]{:S(2)}) copy-start(f32[32,5248]{1,0:T(8,128)} %all-reduce.14.cloned.1.call-done) | copy-start | bytes 2015236
Sparse Core Ops, SparseCore 0:
  105.7 31.8 all-reduce.5
  183.5 83.9 all-reduce.7
  310.8 33.0 all-reduce.9
  394.4 83.9 all-reduce.11
  522.0 33.0 all-reduce.13
